TPU v7x, 32 devices: a whole 2x2x4 slice. The times are simulated.
32 devices in a mesh: rep: 4 (over y, x), fsdp: 2 (over core), tp: 4 (over z).
Axes of the slice: x: 2, y: 2, z: 4, core: 2. Of those that a mesh axis runs over, the one named last changes fastest.
Arguments:
- hidden: bfloat16 [128, 3584], P(('rep', 'fsdp')), may hold values from -6 to 6
- head_weight: bfloat16 [3072, 3584], P(('fsdp', 'tp')), may hold values from -0.09375 to 0.09375
- labels: int32 [128], P(('rep', 'fsdp')), may hold values from 0 to 3071
Outputs:
- grad_hidden: bfloat16 [128, 3584], P(('rep', 'fsdp'), 'tp')
- grad_head: float32 [3072, 3584], P(('fsdp', 'tp', 'rep'))
- token_loss: float32 [128], P(('rep', 'fsdp'))
- top_logprob: float32 [128], P(('rep', 'fsdp'))
- grad_norm: float32 [1], replicated
Inputs may be any that keep to these rules, and one draw needn't show every extreme that they name: labels[t] is a vocabulary index from 0 to 3071, a few indices being very common.
All inputs are finite; a program needn't handle non-finite values.
Results may differ from a plain program's by a relative error of at most 0.0015.
Values may be sent and summed in bfloat16 or wider, within the bound.
A program may use at most 64 MiB of HBM per device.

v0:
```python
import jax
import jax.numpy as jnp
from jax import lax
from jax.sharding import PartitionSpec as P


def merged(part, axis, combine):
    gathered = jax.tree.map(lambda a: lax.all_gather(a, axis), part)

    def take(source):
        return jax.tree.map(lambda a: lax.dynamic_index_in_dim(a, source, 0, False), gathered)

    return lax.fori_loop(
        1, lax.axis_size(axis), lambda source, state: combine(state, take(source)), take(0)
    )


def summed_rows(portion, width, axis):
    count = width * lax.axis_size(axis)
    return lax.psum_scatter(portion(jnp.int32(0), count), axis, scatter_dimension=0, tiled=True)


def combine_stats(first_stats, second_stats):
    row_max = jnp.maximum(first_stats[0], second_stats[0])
    row_sum = first_stats[1] * jnp.exp(first_stats[0] - row_max) + second_stats[1] * jnp.exp(
        second_stats[0] - row_max
    )
    return (row_max, row_sum, first_stats[2] + second_stats[2])


def local(hidden, head_weight, labels):
    vocab_local = head_weight.shape[0]
    own_rows = hidden.shape[0]
    block_index = lax.axis_index("fsdp") * lax.axis_size("tp") + lax.axis_index("tp")
    vocab_start = block_index * vocab_local
    group_labels = lax.all_gather(labels, "fsdp", axis=0, tiled=True)
    group_hidden = lax.all_gather(hidden, "fsdp", axis=0, tiled=True)
    logits = lax.dot_general(
        group_hidden, head_weight, (((1,), (1,)), ((), ())), preferred_element_type=jnp.float32
    )
    local_ids = group_labels - vocab_start
    vocab_ids = lax.broadcasted_iota(jnp.int32, logits.shape, 1)
    chosen = vocab_ids == local_ids[:, None]
    label_part = jnp.sum(jnp.where(chosen, logits, jnp.zeros_like(logits)), axis=1)
    local_max = jnp.max(logits, axis=1)
    local_sum = jnp.sum(jnp.exp(logits - local_max[:, None]), axis=1)
    row_max, row_sum, label_logit = merged(
        (local_max, local_sum, label_part), ("fsdp", "tp"), combine_stats
    )
    log_norm = row_max + jnp.log(row_sum)
    own_start = lax.axis_index("fsdp") * own_rows
    token_loss = lax.dynamic_slice_in_dim(log_norm - label_logit, own_start, own_rows, 0)
    top_logprob = lax.dynamic_slice_in_dim(row_max - log_norm, own_start, own_rows, 0)
    probabilities = jnp.exp(logits - log_norm[:, None])
    grad_logits = (probabilities - chosen.astype(jnp.float32)).astype(jnp.bfloat16)

    def token_term(row_start, row_count):
        grad_rows = lax.dynamic_slice_in_dim(grad_logits, row_start, row_count, 0)
        return jnp.dot(grad_rows, head_weight, preferred_element_type=jnp.float32)

    token_sums = summed_rows(token_term, own_rows, "fsdp")
    grad_hidden = lax.psum_scatter(token_sums, "tp", scatter_dimension=1, tiled=True)
    grad_hidden = grad_hidden.astype(jnp.bfloat16)
    rows_head = vocab_local // lax.axis_size("rep")

    def head_term(row_start, row_count):
        grad_part = lax.dynamic_slice_in_dim(grad_logits, row_start, row_count, 1)
        return lax.dot_general(
            grad_part, group_hidden, (((0,), (0,)), ((), ())), preferred_element_type=jnp.float32
        )

    grad_head = summed_rows(head_term, rows_head, "rep")
    squares = jnp.sum(grad_head * grad_head)
    grad_norm = jnp.sqrt(lax.psum(squares, ("rep", "fsdp", "tp"))).reshape(1)
    return (grad_hidden, grad_head, token_loss, top_logprob, grad_norm)


def solution(mesh):
    in_specs = (P(("rep", "fsdp"), None), P(("fsdp", "tp"), None), P(("rep", "fsdp")))
    out_specs = (
        P(("rep", "fsdp"), "tp"),
        P(("fsdp", "tp", "rep"), None),
        P(("rep", "fsdp")),
        P(("rep", "fsdp")),
        P(),
    )
    return jax.shard_map(local, mesh=mesh, in_specs=in_specs, out_specs=out_specs, check_vma=False)
```

profile of v0, /device:TPU:0, one launch (start us, length us, event | category | flops | bytes accessed | tf_op | source)
XLA Modules:
  0.0 183.3 jit_solution(3275276286572791117)
XLA Ops:
  7.2 1.4 dynamic-slice.2
  8.6 1.2 dynamic-slice
  10.5 0.9 dynamic-update-slice.2
  11.4 2.0 %all-reduce.2 = s32[32]{0:T(128)S(1)} all-reduce(s32[32]{0:T(128)S(1)} %dynamic-update-slice.2), channel_id=1, replica_groups=mesh['rep'=4,'fsdp'=2,'tp'=4] {'fsdp'}, use_global_device_ids=true, to_apply=%add.2 | all-reduce | flops 32 | bytes 256
  13.4 2.2 %all_gather.24 = bf16[32,3584]{1,0:T(8,128)(2,1)S(1)} all-gather(bf16[16,3584]{1,0:T(8,128)(2,1)} %param.5), channel_id=1, replica_groups=mesh['rep'=4,'fsdp'=2,'tp'=4] {'fsdp'}, dimensions={0}, use_global_device_ids=true | all-gather | bytes 344064 | tf_op jit(solution)/shard_map/all_gather | solution.py:37
  16.2 1.0 fusion.11
  17.3 0.2 dynamic-update-slice
  17.5 0.2 select_reduce_fusion
  17.7 0.2 dynamic-update-slice.3
  18.0 0.2 dynamic-update-slice.1
  18.2 18.4 %all-reduce.4 = (f32[256]{0:T(256)S(1)}, f32[256]{0:T(256)S(1)}, f32[256]{0:T(256)S(1)}) all-reduce(f32[256]{0:T(256)S(1)} %dynamic-update-slice, f32[256]{0:T(256)S(1)} %dynamic-update-slice.1, f32[256]{0:T(256)S(1)} %dynamic-update-slice.3), channel_id=2, replica_groups=mesh['rep'=4,'fsdp'=2,'tp'=4] {'fsdp','tp'}, use_global_device_ids=true, to_apply=%add | all-reduce | flops 768 | bytes 6144
  36.5 0.1 reshape.19
  36.6 0.1 reshape.18
  36.8 0.3 while.19
  37.1 1.4 fusion.8
  38.6 3.4 %fusion.7 = f32[384,3584]{1,0:T(8,128)} fusion(bf16[32,3584]{1,0:T(8,128)(2,1)S(1)} %all_gather.24, f32[32,384]{1,0:T(8,128)S(1)} %get-tuple-element.211, f32[32]{0:T(128)S(1)} %get-tuple-element.208, s32[32]{0:T(128)S(1)} %broadcast_subtract_fusion), kind=kOutput, calls=%fused_computation.17 | convolution fusion | flops 88141824 | bytes 5783808 | tf_op jit(solution)/shard_map/dot_general | solution.py:68
  42.0 2.7 %reduce-scatter.4.cloned.1.call-done = f32[16,3584]{1,0:T(8,128)} async-done(((f32[32,3584]{1,0:T(8,128)}), f32[16,3584]{1,0:T(8,128)}) %reduce-scatter.4.cloned.1.call-update) | async-done | bytes 229392 | tf_op jit(solution)/shard_map/reduce_scatter | solution.py:20
  44.8 0.6 dynamic_slice.50
  45.4 0.6 dynamic_slice.49
  46.0 66.8 %reduce-scatter.8.cloned.1.call-done = f32[96,3584]{1,0:T(8,128)} async-done(((f32[384,3584]{1,0:T(8,128)}), f32[96,3584]{1,0:T(8,128)}) %reduce-scatter.8.cloned.1.call-update) | async-done | bytes 1376272 | tf_op jit(solution)/shard_map/reduce_scatter | solution.py:20
  112.8 2.3 %multiply_reduce_fusion = f32[]{:T(128)} fusion(f32[96,3584]{1,0:T(8,128)} %reduce-scatter.8.cloned.1.call-done), kind=kLoop, calls=%fused_computation.10 | loop fusion | flops 688127 | bytes 1376260 | tf_op jit(solution)/shard_map/reduce_sum | solution.py:73
  115.1 19.9 %reduce-scatter.6.cloned.1.call-done = f32[16,896]{1,0:T(8,128)} async-done(((f32[16,3584]{1,0:T(8,128)}), f32[16,896]{1,0:T(8,128)}) %reduce-scatter.6.cloned.1.call-update) | async-done | bytes 57360 | tf_op jit(solution)/shard_map/reduce_scatter | solution.py:62
  135.0 1.4 convert_element_type.11
  136.4 38.5 %psum.7 = f32[]{:T(128)} all-reduce(f32[]{:T(128)} %multiply_reduce_fusion), channel_id=1, replica_groups=mesh['rep'=4,'fsdp'=2,'tp'=4] {'rep','fsdp','tp'}, use_global_device_ids=true, to_apply=%region_9.10 | all-reduce | flops 1 | bytes 8 | tf_op jit(solution)/shard_map/psum | solution.py:74
  (26 shorter events, 0.5 us)
Async XLA Ops:
  7.2 9.0 %copy-start = (bf16[384,3584]{1,0:T(8,128)(2,1)S(1)}, bf16[384,3584]{1,0:T(8,128)(2,1)}, u32[]{:S(2)}) copy-start(bf16[384,3584]{1,0:T(8,128)(2,1)} %param.6) | copy-start | bytes 8257540
  7.2 37.6 %reduce-scatter.4.cloned.1.call-start = ((), (), s32[]{:S(2)}) async-start(), calls=%async_computation.3 | async-start | bytes 688128 | tf_op jit(solution)/shard_map/reduce_scatter | solution.py:20
  38.5 74.3 %reduce-scatter.8.cloned.1.call-start = ((), (), s32[]{:S(2)}) async-start(), calls=%async_computation.5 | async-start | bytes 6881280 | tf_op jit(solution)/shard_map/reduce_scatter | solution.py:20
  42.0 93.0 %reduce-scatter.6.cloned.1.call-start = ((), (), s32[]{:S(2)}) async-start(), calls=%async_computation.4 | async-start | bytes 286720 | tf_op jit(solution)/shard_map/reduce_scatter | solution.py:62
Sparse Core Ops, SparseCore 0:
  38.7 6.0 reduce-scatter.3
  48.4 64.3 reduce-scatter.7
  115.1 19.8 reduce-scatter.5
where the time goes:
time: 184 us; the launch traced here: 183 us
  waiting for transfers between devices  89.5 us (49%)
  blocking collectives  61.1 us (33%)
  between operations  17 us (9%)
  matrix products  5.84 us (3%)
  local copies, waits for them, and re-layouts  5.6 us (3%)
  other arithmetic  4.12 us (2%)
    reduce_scatter x2, waiting for transfers between devices, summed_rows(): lax.psum_scatter(portion(jnp.int32(0), count), axis, scatter_dimension=0,...  69.6 us
    psum x1, blocking collectives, local(): grad_norm = jnp.sqrt(lax.psum(squares, ('rep', 'fsdp', 'tp'))).reshape(1)  38.5 us
    unnamed x2, blocking collectives  20.3 us
    reduce_scatter x1, waiting for transfers between devices, local(): lax.psum_scatter(token_sums, 'tp', scatter_dimension=1, tiled=True)  19.9 us
    unnamed x12, local copies, waits for them, and re-layouts  4.19 us
  transfers between devices with their start and end apart: 3, of which 3 were waited for; matrix products, arithmetic and copies ran while one was open for 4% of the time, Pallas kernels for 0%

commit v1 on v0

v1 whole, which is shorter than its diff:
```python
import functools

import jax
import jax.numpy as jnp
from jax import lax
from jax.experimental import pallas as pl
from jax.experimental.pallas import tpu as pltpu
from jax.sharding import PartitionSpec as P

MESH = pl.DeviceIdType.MESH
LANES = 128


def flipped(values, to_row):
    n = max(values.shape)
    square = (n, n)
    same = lax.broadcasted_iota(jnp.int32, square, 0) == lax.broadcasted_iota(jnp.int32, square, 1)
    spread = jnp.where(same, jnp.broadcast_to(values, square), 0.0)
    return jnp.sum(spread, axis=0 if to_row else 1, keepdims=True)


def kernel(
    R, F, T,
    hidden_hbm, head_hbm, labels_ref,
    gh_ref, grad_head_hbm, loss_ref, top_ref, norm_ref,
    hid, head, labs, logits, stats, gl, gl_send, gl_all,
    part, s1_send, s1_recv, s2_send, s2_recv, gout, nrm1, nrm2,
    in_sem, head_sem, out_sem,
    hs_send, hs_recv, fw_send, fw_recv, ls_send, ls_recv,
    st_send, st_recv, gl_ss, gl_rs, s1_ss, s1_rs, s2_ss, s2_rs,
    n1_ss, n1_rs, n2_ss, n2_rs,
):
    r, f, t = lax.axis_index("rep"), lax.axis_index("fsdp"), lax.axis_index("tp")
    n = hidden_hbm.shape[0]
    vocab, width = head.shape
    own_vocab = vocab // R
    cols = width // T
    group = F * n

    def at(k, a, b):
        return (lax.rem(r + k + R, R), lax.rem(f + a + F, F), lax.rem(t + b + T, T))

    sent = []

    def send(src, dst, ss, rs, where):
        copy = pltpu.make_async_remote_copy(
            src_ref=src, dst_ref=dst, send_sem=ss, recv_sem=rs, device_id=at(*where), device_id_type=MESH
        )
        copy.start()
        sent.append(copy)

    def arrived(dst, ss, rs, where):
        pltpu.make_async_remote_copy(
            src_ref=dst, dst_ref=dst, send_sem=ss, recv_sem=rs, device_id=at(*where), device_id_type=MESH
        ).wait_recv()

    own = pltpu.make_async_copy(hidden_hbm, hid.at[0, 0], in_sem)
    own.start()
    blocks = vocab // LANES
    loads = []
    for i in range(blocks):
        rows = pl.ds(i * LANES, LANES)
        loads.append(pltpu.make_async_copy(head_hbm.at[rows], head.at[rows], head_sem.at[i]))
        loads[-1].start()

    peers = [(k, 0, 0) for k in range(1, R)]
    mates = [(0, a, b) for a in range(F) for b in range(T) if a or b]
    barrier = pltpu.get_barrier_semaphore()
    for where in peers + mates:
        pl.semaphore_signal(barrier, inc=1, device_id=at(*where), device_id_type=MESH)
    pl.semaphore_wait(barrier, len(peers) + len(mates))

    own.wait()
    for a in range(1, F):
        send(labels_ref, labs.at[a - 1], ls_send.at[a - 1], ls_recv.at[a - 1], (0, a, 0))
        send(hid.at[0, 0], hid.at[0, a], hs_send.at[0, a - 1], hs_recv.at[0, a - 1], (0, a, 0))
    for k in range(1, R):
        send(hid.at[0, 0], hid.at[k, 0], fw_send.at[k - 1], fw_recv.at[k - 1], (k, 0, 0))

    for a in range(1, F):
        arrived(labs.at[a - 1], ls_send.at[a - 1], ls_recv.at[a - 1], (0, a, 0))
        arrived(hid.at[0, a], hs_send.at[0, a - 1], hs_recv.at[0, a - 1], (0, a, 0))
    tokens = hid[0].reshape(group, width)
    for i in range(blocks):
        loads[i].wait()
        logits[:, i * LANES : (i + 1) * LANES] = lax.dot_general(
            tokens, head[i * LANES : (i + 1) * LANES, :], (((1,), (1,)), ((), ())),
            preferred_element_type=jnp.float32,
        )

    label_rows = [labels_ref[...]] + [labs[a - 1] for a in range(1, F)]
    label_cols = [flipped(row.astype(jnp.float32), False).astype(jnp.int32) for row in label_rows]
    labels = jnp.concatenate(label_cols, axis=0) if F > 1 else label_cols[0]
    vocab_start = (f * T + t) * vocab
    scores = logits[...]
    chosen = lax.broadcasted_iota(jnp.int32, scores.shape, 1) == labels - vocab_start
    local_max = jnp.max(scores, axis=1, keepdims=True)
    local_sum = jnp.sum(jnp.exp(scores - local_max), axis=1, keepdims=True)
    label_part = jnp.sum(jnp.where(chosen, scores, 0.0), axis=1, keepdims=True)
    lane = lax.broadcasted_iota(jnp.int32, (group, LANES), 1)
    stats[0] = jnp.where(lane == 0, local_max, jnp.where(lane == 1, local_sum, label_part))
    for k, a, b in mates:
        slot = a * T + b
        send(stats.at[0], stats.at[slot], st_send.at[slot - 1], st_recv.at[slot - 1], (0, a, b))

    for k in range(1, R):
        arrived(hid.at[k, 0], fw_send.at[k - 1], fw_recv.at[k - 1], (k, 0, 0))
        for a in range(1, F):
            send(hid.at[k, 0], hid.at[k, a], hs_send.at[k, a - 1], hs_recv.at[k, a - 1], (0, a, 0))

    for k, a, b in mates:
        slot = a * T + b
        arrived(stats.at[slot], st_send.at[slot - 1], st_recv.at[slot - 1], (0, a, b))

    def from_mate(slot):
        a = slot // T
        if a == 0:
            return stats[slot]
        pieces = [stats[slot, ((c - a) % F) * n : ((c - a) % F + 1) * n, :] for c in range(F)]
        return jnp.concatenate(pieces, axis=0)

    tables = [from_mate(slot) for slot in range(F * T)]
    row_max = functools.reduce(jnp.maximum, [table[:, 0:1] for table in tables])
    row_sum = sum(table[:, 1:2] * jnp.exp(table[:, 0:1] - row_max) for table in tables)
    label_logit = sum(table[:, 2:3] for table in tables)
    log_norm = row_max + jnp.log(row_sum)
    grad = jnp.exp(logits[...] - log_norm) - chosen.astype(jnp.float32)
    for k in range(R):
        gl_send[k] = grad[:, k * own_vocab : (k + 1) * own_vocab].astype(jnp.bfloat16)
    gl[...] = grad.astype(jnp.bfloat16)
    for k in range(1, R):
        send(
            gl_send.at[lax.rem(r + k, R)], gl_all.at[k], gl_ss.at[k - 1], gl_rs.at[k - 1], (k, 0, 0)
        )
    gl_all[0] = gl_send[r]

    order = list(range(1, T)) + [0]
    for b in order:
        start = pl.multiple_of(lax.rem(t + b, T) * cols, cols)
        piece = jnp.dot(gl[...], head[:, pl.ds(start, cols)], preferred_element_type=jnp.float32)
        part[b] = piece[:n]
        for a in range(1, F):
            s1_send[a - 1, b] = piece[a * n : (a + 1) * n]
            send(
                s1_send.at[a - 1, b], s1_recv.at[a - 1, b], s1_ss.at[a - 1, b], s1_rs.at[a - 1, b],
                (0, -a, 0),
            )
    for b in order:
        total = part[b]
        for a in range(1, F):
            arrived(s1_recv.at[a - 1, b], s1_ss.at[a - 1, b], s1_rs.at[a - 1, b], (0, a, 0))
            total = total + s1_recv[a - 1, b]
        if b:
            s2_send[b - 1] = total
            send(s2_send.at[b - 1], s2_recv.at[b - 1], s2_ss.at[b - 1], s2_rs.at[b - 1], (0, 0, b))
        else:
            part[0] = total

    own_loss = flipped((log_norm - label_logit)[:n], True)
    loss_ref[...] = own_loss
    top_ref[...] = flipped((row_max - log_norm)[:n], True)

    for k in range(1, R):
        arrived(gl_all.at[k], gl_ss.at[k - 1], gl_rs.at[k - 1], (k, 0, 0))
        for a in range(1, F):
            arrived(hid.at[k, a], hs_send.at[k, a - 1], hs_recv.at[k, a - 1], (0, a, 0))
    all_gl = gl_all[...].reshape(R * group, own_vocab)
    squares = jnp.zeros((8, cols), jnp.float32)
    outs = []
    for b in range(T):
        span = slice(b * cols, (b + 1) * cols)
        piece = lax.dot_general(
            all_gl, hid[:, :, :, span].reshape(R * group, cols), (((0,), (0,)), ((), ())),
            preferred_element_type=jnp.float32,
        )
        gout[:, span] = piece
        outs.append(pltpu.make_async_copy(gout.at[:, span], grad_head_hbm.at[:, span], out_sem.at[b]))
        outs[-1].start()
        squares = squares + jnp.sum((piece * piece).reshape(own_vocab // 8, 8, cols), axis=0)
    nrm1[0] = sum(squares[:, i * LANES : (i + 1) * LANES] for i in range(cols // LANES))
    for k in range(1, R):
        send(nrm1.at[0], nrm1.at[k], n1_ss.at[k - 1], n1_rs.at[k - 1], (k, 0, 0))
    for k in range(1, R):
        arrived(nrm1.at[k], n1_ss.at[k - 1], n1_rs.at[k - 1], (k, 0, 0))
    nrm2[0] = jnp.sum(nrm1[...], axis=0)
    for k, a, b in mates:
        slot = a * T + b
        send(nrm2.at[0], nrm2.at[slot], n2_ss.at[slot - 1], n2_rs.at[slot - 1], (0, a, b))

    total = part[0]
    for b in range(1, T):
        arrived(s2_recv.at[b - 1], s2_ss.at[b - 1], s2_rs.at[b - 1], (0, 0, b))
        total = total + s2_recv[b - 1]
    gh_ref[...] = total.astype(jnp.bfloat16)

    for k, a, b in mates:
        slot = a * T + b
        arrived(nrm2.at[slot], n2_ss.at[slot - 1], n2_rs.at[slot - 1], (0, a, b))
    lanes = jnp.sum(jnp.sum(nrm2[...], axis=0), axis=0, keepdims=True)
    norm_ref[...] = jnp.sqrt(jnp.sum(lanes, axis=1, keepdims=True))

    for copy in sent:
        copy.wait_send()
    for copy in outs:
        copy.wait()


def local(R, F, T, hidden, head_weight, labels):
    n, width = hidden.shape
    vocab = head_weight.shape[0]
    own_vocab = vocab // R
    cols = width // T
    group = F * n
    f32, bf16 = jnp.float32, jnp.bfloat16
    dma = pltpu.SemaphoreType.DMA
    vmem = pl.BlockSpec(memory_space=pltpu.VMEM)
    hbm = pl.BlockSpec(memory_space=pl.ANY)
    FM = max(F - 1, 1)
    slots = F * T
    scratch = [
        pltpu.VMEM((R, F, n, width), bf16),
        pltpu.VMEM((vocab, width), bf16),
        pltpu.VMEM((FM, 1, n), jnp.int32),
        pltpu.VMEM((group, vocab), f32),
        pltpu.VMEM((slots, group, LANES), f32),
        pltpu.VMEM((group, vocab), bf16),
        pltpu.VMEM((R, group, own_vocab), bf16),
        pltpu.VMEM((R, group, own_vocab), bf16),
        pltpu.VMEM((T, n, cols), f32),
        pltpu.VMEM((FM, T, n, cols), f32),
        pltpu.VMEM((FM, T, n, cols), f32),
        pltpu.VMEM((T - 1, n, cols), f32),
        pltpu.VMEM((T - 1, n, cols), f32),
        pltpu.VMEM((own_vocab, width), f32),
        pltpu.VMEM((R, 8, LANES), f32),
        pltpu.VMEM((slots, 8, LANES), f32),
        dma(()), dma((vocab // LANES,)), dma((T,)),
        dma((R, FM)), dma((R, FM)), dma((R - 1,)), dma((R - 1,)), dma((FM,)), dma((FM,)),
        dma((slots - 1,)), dma((slots - 1,)), dma((R - 1,)), dma((R - 1,)),
        dma((FM, T)), dma((FM, T)), dma((T - 1,)), dma((T - 1,)),
        dma((R - 1,)), dma((R - 1,)), dma((slots - 1,)), dma((slots - 1,)),
    ]
    grad_hidden, grad_head, loss, top, norm = pl.pallas_call(
        functools.partial(kernel, R, F, T),
        out_shape=(
            jax.ShapeDtypeStruct((n, cols), bf16),
            jax.ShapeDtypeStruct((own_vocab, width), f32),
            jax.ShapeDtypeStruct((1, n), f32),
            jax.ShapeDtypeStruct((1, n), f32),
            jax.ShapeDtypeStruct((1, 1), f32),
        ),
        in_specs=[hbm, hbm, vmem],
        out_specs=(vmem, hbm, vmem, vmem, vmem),
        scratch_shapes=scratch,
        compiler_params=pltpu.CompilerParams(
            collective_id=0, has_side_effects=True, vmem_limit_bytes=60 * 1024 * 1024
        ),
    )(hidden, head_weight, labels.reshape(1, n))
    return (grad_hidden, grad_head, loss.reshape(n), top.reshape(n), norm.reshape(1))


def solution(mesh):
    in_specs = (P(("rep", "fsdp"), None), P(("fsdp", "tp"), None), P(("rep", "fsdp")))
    out_specs = (
        P(("rep", "fsdp"), "tp"),
        P(("fsdp", "tp", "rep"), None),
        P(("rep", "fsdp")),
        P(("rep", "fsdp")),
        P(),
    )
    body = functools.partial(local, mesh.shape["rep"], mesh.shape["fsdp"], mesh.shape["tp"])
    return jax.shard_map(body, mesh=mesh, in_specs=in_specs, out_specs=out_specs, check_vma=False)
```

time: 184 us -> 33.2 us (0.18)
  waiting for transfers between devices: 89.5 us -> 0 us
  blocking collectives: 61.1 us -> 0 us
  Pallas kernels: 0 us -> 25.7 us
  between operations: 17 us -> 2.39 us
  matrix products: 5.84 us -> 0 us
  other arithmetic: 4.12 us -> 0 us
    reduce_scatter x3 -> x0, waiting for transfers between devices: 89.4 us -> none  [the longest x2 69.6 us: summed_rows(): lax.psum_scatter(portion(jnp.int32(0), count), axis, scatter_dimension=0,...]
    psum x1 -> x0, blocking collectives: 38.5 us -> none  [local(): grad_norm = jnp.sqrt(lax.psum(squares, ('rep', 'fsdp', 'tp'))).reshape(1)]
    pallas_call x0 -> x1, Pallas kernels: none -> 25.7 us  [local(): pl.pallas_call(functools.partial(kernel, R, F, T), out_shape=(jax.ShapeDt...]
    unnamed x2 -> x0, blocking collectives: 20.3 us -> none
    dot_general x3 -> x0, matrix products: 5.84 us -> none  [the longest x1 3.36 us: head_term(): lax.dot_general(grad_part, group_hidden, (((0,), (0,)), ((), ())), prefer...]
    reduce_sum x2 -> x0, other arithmetic: 2.49 us -> none  [the longest x1 2.3 us: local(): squares = jnp.sum(grad_head * grad_head)]
    all_gather x1 -> x0, blocking collectives: 2.17 us -> none  [local(): group_hidden = lax.all_gather(hidden, 'fsdp', axis=0, tiled=True)]
    unnamed x12 -> x8, local copies, waits for them, and re-layouts: 4.19 us -> 4.9 us
  transfers between devices with their start and end apart: 3 -> 0, of which waited for: 3 -> 0; matrix products, arithmetic and copies ran while one was open for 4% -> 0% of each run, Pallas kernels for 0% -> 0%
where the time goes in v1:
time: 33.2 us; the launch traced here: 33 us
  Pallas kernels  25.7 us (77%)
  local copies, waits for them, and re-layouts  4.9 us (15%)
  between operations  2.39 us (7%)
    pallas_call x1, Pallas kernels, local(): pl.pallas_call(functools.partial(kernel, R, F, T), out_shape=(jax.ShapeDt...  25.7 us
    unnamed x8, local copies, waits for them, and re-layouts  4.9 us

profile of v1, /device:TPU:0, one launch (start us, length us, event | category | flops | bytes accessed | tf_op | source)
XLA Modules:
  0.0 33.0 jit_solution(4152079537881366243)
XLA Ops:
  0.6 25.7 %shard_map.74 = (bf16[16,896]{1,0:T(8,128)(2,1)}, f32[96,3584]{1,0:T(8,128)}, f32[1,16]{1,0:T(1,128)}, f32[1,16]{1,0:T(1,128)}, f32[1,1]{1,0:T(1,128)}) custom-call(bf16[16,3584]{1,0:T(8,128)(2,1)} %hidden_hbm.1, bf16[384,3584]{1,0:T(8,128)(2,1)} %head_hbm.1, s32[1,16]{1,0:T(1,128)} %bitcast.4), custom_call_target="tpu_custom_call" | custom-call | tf_op jit(solution)/shard_map/pallas_call | solution.py:243
  26.4 1.4 %copy.13 = bf16[16,896]{1,0:T(8,128)(2,1)} copy(bf16[16,896]{1,0:T(8,128)(2,1)} %get-tuple-element.20) | data formatting | bytes 57344
  27.7 0.0 copy-start.1
  27.7 0.0 copy-start
  27.7 2.5 %copy.14 = f32[96,3584]{1,0:T(8,128)} copy(f32[96,3584]{1,0:T(8,128)} %get-tuple-element.21) | data formatting | bytes 2752512
  30.2 0.0 copy-done.1
  30.2 0.5 %copy.15 = f32[16]{0:T(128)} copy(f32[16]{0:T(128)S(1)} %bitcast.6) | data formatting | bytes 128
  30.7 0.0 copy-done
  30.7 0.5 %copy.16 = f32[16]{0:T(128)} copy(f32[16]{0:T(128)S(1)} %bitcast.5) | data formatting | bytes 128
Async XLA Ops:
  27.7 2.5 %copy-start.1 = (f32[1,16]{1,0:T(1,128)S(1)}, f32[1,16]{1,0:T(1,128)}, u32[]{:S(2)}) copy-start(f32[1,16]{1,0:T(1,128)} %get-tuple-element.12) | copy-start | bytes 196
  27.7 3.0 %copy-start = (f32[1,16]{1,0:T(1,128)S(1)}, f32[1,16]{1,0:T(1,128)}, u32[]{:S(2)}) copy-start(f32[1,16]{1,0:T(1,128)} %get-tuple-element.13) | copy-start | bytes 196

commit v2 on v1

--- a/solution.py
+++ b/solution.py
@@ -22,10 +22,10 @@
 def kernel(
     R, F, T,
     hidden_hbm, head_hbm, labels_ref,
-    gh_ref, grad_head_hbm, loss_ref, top_ref, norm_ref,
-    hid, head, labs, logits, stats, gl, gl_send, gl_all,
-    part, s1_send, s1_recv, s2_send, s2_recv, gout, nrm1, nrm2,
-    in_sem, head_sem, out_sem,
+    gh_ref, gout, loss_ref, top_ref, norm_ref,
+    hid, head, labs, logits, stats_send, stats, gl, gl_send, gl_all,
+    part, s1_send, s1_recv, s2_send, s2_recv, nrm1, nrm2,
+    in_sem, head_sem,
     hs_send, hs_recv, fw_send, fw_recv, ls_send, ls_recv,
     st_send, st_recv, gl_ss, gl_rs, s1_ss, s1_rs, s2_ss, s2_rs,
     n1_ss, n1_rs, n2_ss, n2_rs,
@@ -98,10 +98,14 @@
     local_sum = jnp.sum(jnp.exp(scores - local_max), axis=1, keepdims=True)
     label_part = jnp.sum(jnp.where(chosen, scores, 0.0), axis=1, keepdims=True)
     lane = lax.broadcasted_iota(jnp.int32, (group, LANES), 1)
-    stats[0] = jnp.where(lane == 0, local_max, jnp.where(lane == 1, local_sum, label_part))
-    for k, a, b in mates:
-        slot = a * T + b
-        send(stats.at[0], stats.at[slot], st_send.at[slot - 1], st_recv.at[slot - 1], (0, a, b))
+    packed = jnp.where(lane == 0, local_max, jnp.where(lane == 1, local_sum, label_part))
+    for a in range(F):
+        turned = packed if a == 0 else jnp.concatenate([packed[(F - a) * n :], packed[: (F - a) * n]], axis=0)
+        stats_send[a] = turned.T[:8]
+    for k, a, b in mates:
+        slot = a * T + b
+        send(stats_send.at[a], stats.at[slot], st_send.at[slot - 1], st_recv.at[slot - 1], (0, a, b))
+    stats[0] = stats_send[0]
 
     for k in range(1, R):
         arrived(hid.at[k, 0], fw_send.at[k - 1], fw_recv.at[k - 1], (k, 0, 0))
@@ -111,19 +115,12 @@
     for k, a, b in mates:
         slot = a * T + b
         arrived(stats.at[slot], st_send.at[slot - 1], st_recv.at[slot - 1], (0, a, b))
-
-    def from_mate(slot):
-        a = slot // T
-        if a == 0:
-            return stats[slot]
-        pieces = [stats[slot, ((c - a) % F) * n : ((c - a) % F + 1) * n, :] for c in range(F)]
-        return jnp.concatenate(pieces, axis=0)
-
-    tables = [from_mate(slot) for slot in range(F * T)]
-    row_max = functools.reduce(jnp.maximum, [table[:, 0:1] for table in tables])
-    row_sum = sum(table[:, 1:2] * jnp.exp(table[:, 0:1] - row_max) for table in tables)
-    label_logit = sum(table[:, 2:3] for table in tables)
-    log_norm = row_max + jnp.log(row_sum)
+    tables = [stats[slot] for slot in range(F * T)]
+    row_max = functools.reduce(jnp.maximum, [table[0:1] for table in tables])
+    row_sum = sum(table[1:2] * jnp.exp(table[0:1] - row_max) for table in tables)
+    label_logit = sum(table[2:3] for table in tables)
+    log_row = row_max + jnp.log(row_sum)
+    log_norm = flipped(log_row, False)
     grad = jnp.exp(logits[...] - log_norm) - chosen.astype(jnp.float32)
     for k in range(R):
         gl_send[k] = grad[:, k * own_vocab : (k + 1) * own_vocab].astype(jnp.bfloat16)
@@ -156,9 +153,8 @@
         else:
             part[0] = total
 
-    own_loss = flipped((log_norm - label_logit)[:n], True)
-    loss_ref[...] = own_loss
-    top_ref[...] = flipped((row_max - log_norm)[:n], True)
+    loss_ref[...] = (log_row - label_logit)[:, :n]
+    top_ref[...] = (row_max - log_row)[:, :n]
 
     for k in range(1, R):
         arrived(gl_all.at[k], gl_ss.at[k - 1], gl_rs.at[k - 1], (k, 0, 0))
@@ -166,7 +162,6 @@
             arrived(hid.at[k, a], hs_send.at[k, a - 1], hs_recv.at[k, a - 1], (0, a, 0))
     all_gl = gl_all[...].reshape(R * group, own_vocab)
     squares = jnp.zeros((8, cols), jnp.float32)
-    outs = []
     for b in range(T):
         span = slice(b * cols, (b + 1) * cols)
         piece = lax.dot_general(
@@ -174,8 +169,6 @@
             preferred_element_type=jnp.float32,
         )
         gout[:, span] = piece
-        outs.append(pltpu.make_async_copy(gout.at[:, span], grad_head_hbm.at[:, span], out_sem.at[b]))
-        outs[-1].start()
         squares = squares + jnp.sum((piece * piece).reshape(own_vocab // 8, 8, cols), axis=0)
     nrm1[0] = sum(squares[:, i * LANES : (i + 1) * LANES] for i in range(cols // LANES))
     for k in range(1, R):
@@ -201,7 +194,18 @@
 
     for copy in sent:
         copy.wait_send()
-    for copy in outs:
+
+
+def store(*refs):
+    count = (len(refs) - 1) // 2
+    sources, targets, sems = refs[:count], refs[count : 2 * count], refs[-1]
+    copies = [
+        pltpu.make_async_copy(sources[i], targets[i], sems.at[i]) for i in range(count - 1)
+    ]
+    for copy in copies:
+        copy.start()
+    targets[-1][...] = sources[-1][...]
+    for copy in copies:
         copy.wait()
 
 
@@ -214,7 +218,8 @@
     f32, bf16 = jnp.float32, jnp.bfloat16
     dma = pltpu.SemaphoreType.DMA
     vmem = pl.BlockSpec(memory_space=pltpu.VMEM)
-    hbm = pl.BlockSpec(memory_space=pl.ANY)
+    anywhere = pl.BlockSpec(memory_space=pl.ANY)
+    hbm = pl.BlockSpec(memory_space=pltpu.HBM)
     FM = max(F - 1, 1)
     slots = F * T
     scratch = [
@@ -222,7 +227,8 @@
         pltpu.VMEM((vocab, width), bf16),
         pltpu.VMEM((FM, 1, n), jnp.int32),
         pltpu.VMEM((group, vocab), f32),
-        pltpu.VMEM((slots, group, LANES), f32),
+        pltpu.VMEM((F, 8, group), f32),
+        pltpu.VMEM((slots, 8, group), f32),
         pltpu.VMEM((group, vocab), bf16),
         pltpu.VMEM((R, group, own_vocab), bf16),
         pltpu.VMEM((R, group, own_vocab), bf16),
@@ -231,31 +237,34 @@
         pltpu.VMEM((FM, T, n, cols), f32),
         pltpu.VMEM((T - 1, n, cols), f32),
         pltpu.VMEM((T - 1, n, cols), f32),
-        pltpu.VMEM((own_vocab, width), f32),
         pltpu.VMEM((R, 8, LANES), f32),
         pltpu.VMEM((slots, 8, LANES), f32),
-        dma(()), dma((vocab // LANES,)), dma((T,)),
+        dma(()), dma((vocab // LANES,)),
         dma((R, FM)), dma((R, FM)), dma((R - 1,)), dma((R - 1,)), dma((FM,)), dma((FM,)),
         dma((slots - 1,)), dma((slots - 1,)), dma((R - 1,)), dma((R - 1,)),
         dma((FM, T)), dma((FM, T)), dma((T - 1,)), dma((T - 1,)),
         dma((R - 1,)), dma((R - 1,)), dma((slots - 1,)), dma((slots - 1,)),
     ]
-    grad_hidden, grad_head, loss, top, norm = pl.pallas_call(
+    shapes = [((n, cols), bf16), ((own_vocab, width), f32), ((1, n), f32), ((1, n), f32), ((1, 1), f32)]
+    grant = 67_043_328 - 4 * own_vocab * width - 2 * n * cols - 32 * 1024
+    held = pl.pallas_call(
         functools.partial(kernel, R, F, T),
-        out_shape=(
-            jax.ShapeDtypeStruct((n, cols), bf16),
-            jax.ShapeDtypeStruct((own_vocab, width), f32),
-            jax.ShapeDtypeStruct((1, n), f32),
-            jax.ShapeDtypeStruct((1, n), f32),
-            jax.ShapeDtypeStruct((1, 1), f32),
-        ),
+        out_shape=tuple(pltpu.VMEM(shape, dtype) for shape, dtype in shapes),
         in_specs=[hbm, hbm, vmem],
-        out_specs=(vmem, hbm, vmem, vmem, vmem),
+        out_specs=(vmem,) * 5,
         scratch_shapes=scratch,
         compiler_params=pltpu.CompilerParams(
-            collective_id=0, has_side_effects=True, vmem_limit_bytes=60 * 1024 * 1024
+            collective_id=0, has_side_effects=True, vmem_limit_bytes=grant
         ),
     )(hidden, head_weight, labels.reshape(1, n))
+    grad_hidden, grad_head, loss, top, norm = pl.pallas_call(
+        store,
+        out_shape=tuple(jax.ShapeDtypeStruct(shape, dtype) for shape, dtype in shapes),
+        in_specs=[anywhere] * 4 + [vmem],
+        out_specs=(hbm,) * 4 + (vmem,),
+        scratch_shapes=[dma((4,))],
+        compiler_params=pltpu.CompilerParams(vmem_limit_bytes=1024 * 1024),
+    )(*held)
     return (grad_hidden, grad_head, loss.reshape(n), top.reshape(n), norm.reshape(1))
 
 

time: 33.2 us -> 27.4 us (0.83)
  local copies, waits for them, and re-layouts: 4.9 us -> 0 us
  between operations: 2.39 us -> 0.64 us
  Pallas kernels: 25.7 us -> 26.6 us
    unnamed x8 -> x0, local copies, waits for them, and re-layouts: 4.9 us -> none
    pallas_call x1 -> x2, Pallas kernels: 25.7 us -> 26.6 us  [the longest x1 24.3 us: local(): pl.pallas_call(functools.partial(kernel, R, F, T), out_shape=tuple((pltpu...]
where the time goes in v2:
time: 27.4 us; the launch traced here: 27.2 us
  Pallas kernels  26.6 us (97%)
  between operations  0.64 us (2%)
    pallas_call x1, Pallas kernels, local(): pl.pallas_call(functools.partial(kernel, R, F, T), out_shape=tuple((pltpu...  24.3 us
    pallas_call x1, Pallas kernels, local(): pl.pallas_call(store, out_shape=tuple((jax.ShapeDtypeStruct(shape, dtype)...  2.27 us

profile of v2, /device:TPU:0, one launch (start us, length us, event | category | flops | bytes accessed | tf_op | source)
XLA Modules:
  0.0 27.2 jit_solution(6175558052737717529)
XLA Ops:
  0.6 24.3 %shard_map.74 = (bf16[16,896]{1,0:T(8,128)(2,1)S(1)}, f32[96,3584]{1,0:T(8,128)S(1)}, f32[1,16]{1,0:T(1,128)S(1)}, f32[1,16]{1,0:T(1,128)S(1)}, f32[1,1]{1,0:T(1,128)}) custom-call(bf16[16,3584]{1,0:T(8,128)(2,1)} %hidden_hbm.1, bf16[384,3584]{1,0:T(8,128)(2,1)} %head_hbm.1, s32[1,16]{1,0:T(1,128)} %bitcast.4), custom_call_target="tpu_custom_call" | custom-call | tf_op jit(solution)/shard_map/pallas_call | solution.py:250
  24.9 2.3 %shard_map.75 = (bf16[16,896]{1,0:T(8,128)(2,1)}, f32[96,3584]{1,0:T(8,128)}, f32[1,16]{1,0:T(1,128)}, f32[1,16]{1,0:T(1,128)}, f32[1,1]{1,0:T(1,128)}) custom-call(bf16[16,896]{1,0:T(8,128)(2,1)S(1)} %get-tuple-element.15.refs_0_, f32[96,3584]{1,0:T(8,128)S(1)} %get-tuple-element.16.refs_1_, f32[1,16]{1,0:T(1,128)S(1)} %get-tuple-element.17.refs_2_, ...), custom_call_target="tpu_custom_call" | custom-call | tf_op jit(solution)/shard_map/pallas_call | solution.py:260

commit v3 on v2

--- a/solution.py
+++ b/solution.py
@@ -38,7 +38,11 @@
     group = F * n
 
     def at(k, a, b):
-        return (lax.rem(r + k + R, R), lax.rem(f + a + F, F), lax.rem(t + b + T, T))
+        if R == 4 and k:
+            rep = (r, r + 1 - 2 * lax.rem(r, 2), lax.rem(r + 2, 4), 3 - r)[k]
+        else:
+            rep = lax.rem(r + k, R)
+        return (rep, lax.rem(f + a + F, F), lax.rem(t + b + T, T))
 
     sent = []
 
@@ -74,8 +78,22 @@
     for a in range(1, F):
         send(labels_ref, labs.at[a - 1], ls_send.at[a - 1], ls_recv.at[a - 1], (0, a, 0))
         send(hid.at[0, 0], hid.at[0, a], hs_send.at[0, a - 1], hs_recv.at[0, a - 1], (0, a, 0))
-    for k in range(1, R):
-        send(hid.at[0, 0], hid.at[k, 0], fw_send.at[k - 1], fw_recv.at[k - 1], (k, 0, 0))
+    halves = [pl.ds(0, width // 2), pl.ds(width // 2, width // 2)]
+
+    def pass_on(source, k, h, to):
+        send(
+            hid.at[source, 0, :, halves[h]], hid.at[k, 0, :, halves[h]],
+            fw_send.at[k - 1, h], fw_recv.at[k - 1, h], (to, 0, 0),
+        )
+
+    def landed(k, h):
+        arrived(hid.at[k, 0, :, halves[h]], fw_send.at[k - 1, h], fw_recv.at[k - 1, h], (k, 0, 0))
+
+    relays = [(1, 0, 2), (2, 1, 1)] if R == 4 else []
+    direct = 3 if relays else R
+    for k in range(1, direct):
+        for h in (0, 1) if k == 1 else (1, 0):
+            pass_on(0, k, h, k)
 
     for a in range(1, F):
         arrived(labs.at[a - 1], ls_send.at[a - 1], ls_recv.at[a - 1], (0, a, 0))
@@ -107,10 +125,9 @@
         send(stats_send.at[a], stats.at[slot], st_send.at[slot - 1], st_recv.at[slot - 1], (0, a, b))
     stats[0] = stats_send[0]
 
-    for k in range(1, R):
-        arrived(hid.at[k, 0], fw_send.at[k - 1], fw_recv.at[k - 1], (k, 0, 0))
-        for a in range(1, F):
-            send(hid.at[k, 0], hid.at[k, a], hs_send.at[k, a - 1], hs_recv.at[k, a - 1], (0, a, 0))
+    for k, h, to in relays:
+        landed(k, h)
+        pass_on(k, 3, h, to)
 
     for k, a, b in mates:
         slot = a * T + b
@@ -127,7 +144,7 @@
     gl[...] = grad.astype(jnp.bfloat16)
     for k in range(1, R):
         send(
-            gl_send.at[lax.rem(r + k, R)], gl_all.at[k], gl_ss.at[k - 1], gl_rs.at[k - 1], (k, 0, 0)
+            gl_send.at[at(k, 0, 0)[0]], gl_all.at[k], gl_ss.at[k - 1], gl_rs.at[k - 1], (k, 0, 0)
         )
     gl_all[0] = gl_send[r]
 
@@ -152,6 +169,13 @@
             send(s2_send.at[b - 1], s2_recv.at[b - 1], s2_ss.at[b - 1], s2_rs.at[b - 1], (0, 0, b))
         else:
             part[0] = total
+
+    for k in range(1, R):
+        for h in range(2):
+            if all((k, h) != relay[:2] for relay in relays):
+                landed(k, h)
+        for a in range(1, F):
+            send(hid.at[k, 0], hid.at[k, a], hs_send.at[k, a - 1], hs_recv.at[k, a - 1], (0, a, 0))
 
     loss_ref[...] = (log_row - label_logit)[:, :n]
     top_ref[...] = (row_max - log_row)[:, :n]
@@ -240,7 +264,7 @@
         pltpu.VMEM((R, 8, LANES), f32),
         pltpu.VMEM((slots, 8, LANES), f32),
         dma(()), dma((vocab // LANES,)),
-        dma((R, FM)), dma((R, FM)), dma((R - 1,)), dma((R - 1,)), dma((FM,)), dma((FM,)),
+        dma((R, FM)), dma((R, FM)), dma((R - 1, 2)), dma((R - 1, 2)), dma((FM,)), dma((FM,)),
         dma((slots - 1,)), dma((slots - 1,)), dma((R - 1,)), dma((R - 1,)),
         dma((FM, T)), dma((FM, T)), dma((T - 1,)), dma((T - 1,)),
         dma((R - 1,)), dma((R - 1,)), dma((slots - 1,)), dma((slots - 1,)),

time: 27.4 us -> 28.5 us (1.040)
  Pallas kernels: 26.6 us -> 27.7 us
    pallas_call x1, Pallas kernels: 24.3 us -> 25.4 us  [local(): pl.pallas_call(functools.partial(kernel, R, F, T), out_shape=tuple((pltpu...]
where the time goes in v3:
time: 28.5 us; the launch traced here: 28.3 us
  Pallas kernels  27.7 us (97%)
  between operations  0.64 us (2%)
    pallas_call x1, Pallas kernels, local(): pl.pallas_call(functools.partial(kernel, R, F, T), out_shape=tuple((pltpu...  25.4 us
    pallas_call x1, Pallas kernels, local(): pl.pallas_call(store, out_shape=tuple((jax.ShapeDtypeStruct(shape, dtype)...  2.27 us

profile of v3, /device:TPU:0, one launch (start us, length us, event | category | flops | bytes accessed | tf_op | source)
XLA Modules:
  0.0 28.3 jit_solution(9063904274043840622)
XLA Ops:
  0.6 25.4 %shard_map.74 = (bf16[16,896]{1,0:T(8,128)(2,1)S(1)}, f32[96,3584]{1,0:T(8,128)S(1)}, f32[1,16]{1,0:T(1,128)S(1)}, f32[1,16]{1,0:T(1,128)S(1)}, f32[1,1]{1,0:T(1,128)}) custom-call(bf16[16,3584]{1,0:T(8,128)(2,1)} %hidden_hbm.1, bf16[384,3584]{1,0:T(8,128)(2,1)} %head_hbm.1, s32[1,16]{1,0:T(1,128)} %bitcast.4), custom_call_target="tpu_custom_call" | custom-call | tf_op jit(solution)/shard_map/pallas_call | solution.py:274
  26.0 2.3 %shard_map.75 = (bf16[16,896]{1,0:T(8,128)(2,1)}, f32[96,3584]{1,0:T(8,128)}, f32[1,16]{1,0:T(1,128)}, f32[1,16]{1,0:T(1,128)}, f32[1,1]{1,0:T(1,128)}) custom-call(bf16[16,896]{1,0:T(8,128)(2,1)S(1)} %get-tuple-element.15.refs_0_, f32[96,3584]{1,0:T(8,128)S(1)} %get-tuple-element.16.refs_1_, f32[1,16]{1,0:T(1,128)S(1)} %get-tuple-element.17.refs_2_, ...), custom_call_target="tpu_custom_call" | custom-call | tf_op jit(solution)/shard_map/pallas_call | solution.py:284

commit v4 on v2

--- a/solution.py
+++ b/solution.py
@@ -63,6 +63,14 @@
         loads.append(pltpu.make_async_copy(head_hbm.at[rows], head.at[rows], head_sem.at[i]))
         loads[-1].start()
 
+    def score_block(i, first, last):
+        rows = slice(first * n, last * n)
+        block = lax.dot_general(
+            head[i * LANES : (i + 1) * LANES, :], hid[0, first:last].reshape((last - first) * n, width),
+            (((1,), (1,)), ((), ())), preferred_element_type=jnp.float32,
+        )
+        logits[rows, i * LANES : (i + 1) * LANES] = block.T
+
     peers = [(k, 0, 0) for k in range(1, R)]
     mates = [(0, a, b) for a in range(F) for b in range(T) if a or b]
     barrier = pltpu.get_barrier_semaphore()
@@ -80,13 +88,9 @@
     for a in range(1, F):
         arrived(labs.at[a - 1], ls_send.at[a - 1], ls_recv.at[a - 1], (0, a, 0))
         arrived(hid.at[0, a], hs_send.at[0, a - 1], hs_recv.at[0, a - 1], (0, a, 0))
-    tokens = hid[0].reshape(group, width)
     for i in range(blocks):
         loads[i].wait()
-        logits[:, i * LANES : (i + 1) * LANES] = lax.dot_general(
-            tokens, head[i * LANES : (i + 1) * LANES, :], (((1,), (1,)), ((), ())),
-            preferred_element_type=jnp.float32,
-        )
+        score_block(i, 0, F)
 
     label_rows = [labels_ref[...]] + [labs[a - 1] for a in range(1, F)]
     label_cols = [flipped(row.astype(jnp.float32), False).astype(jnp.int32) for row in label_rows]
@@ -170,7 +174,8 @@
         )
         gout[:, span] = piece
         squares = squares + jnp.sum((piece * piece).reshape(own_vocab // 8, 8, cols), axis=0)
-    nrm1[0] = sum(squares[:, i * LANES : (i + 1) * LANES] for i in range(cols // LANES))
+    lanes = sum(squares[:, i * LANES : (i + 1) * LANES] for i in range(cols // LANES))
+    nrm1[0] = jnp.sum(lanes, axis=0, keepdims=True)
     for k in range(1, R):
         send(nrm1.at[0], nrm1.at[k], n1_ss.at[k - 1], n1_rs.at[k - 1], (k, 0, 0))
     for k in range(1, R):
@@ -189,7 +194,7 @@
     for k, a, b in mates:
         slot = a * T + b
         arrived(nrm2.at[slot], n2_ss.at[slot - 1], n2_rs.at[slot - 1], (0, a, b))
-    lanes = jnp.sum(jnp.sum(nrm2[...], axis=0), axis=0, keepdims=True)
+    lanes = jnp.sum(nrm2[...], axis=0)
     norm_ref[...] = jnp.sqrt(jnp.sum(lanes, axis=1, keepdims=True))
 
     for copy in sent:
@@ -237,8 +242,8 @@
         pltpu.VMEM((FM, T, n, cols), f32),
         pltpu.VMEM((T - 1, n, cols), f32),
         pltpu.VMEM((T - 1, n, cols), f32),
-        pltpu.VMEM((R, 8, LANES), f32),
-        pltpu.VMEM((slots, 8, LANES), f32),
+        pltpu.VMEM((R, 1, LANES), f32),
+        pltpu.VMEM((slots, 1, LANES), f32),
         dma(()), dma((vocab // LANES,)),
         dma((R, FM)), dma((R, FM)), dma((R - 1,)), dma((R - 1,)), dma((FM,)), dma((FM,)),
         dma((slots - 1,)), dma((slots - 1,)), dma((R - 1,)), dma((R - 1,)),

time: 27.4 us -> 27.3 us (level)
  no operation moved by 1% of the time
where the time goes in v4:
time: 27.3 us; the launch traced here: 27.1 us
  Pallas kernels  26.5 us (97%)
  between operations  0.64 us (2%)
    pallas_call x1, Pallas kernels, local(): pl.pallas_call(functools.partial(kernel, R, F, T), out_shape=tuple((pltpu...  24.2 us
    pallas_call x1, Pallas kernels, local(): pl.pallas_call(store, out_shape=tuple((jax.ShapeDtypeStruct(shape, dtype)...  2.27 us

profile of v4, /device:TPU:0, one launch (start us, length us, event | category | flops | bytes accessed | tf_op | source)
XLA Modules:
  0.0 27.1 jit_solution(14829221578233122920)
XLA Ops:
  0.6 24.2 %shard_map.74 = (bf16[16,896]{1,0:T(8,128)(2,1)S(1)}, f32[96,3584]{1,0:T(8,128)S(1)}, f32[1,16]{1,0:T(1,128)S(1)}, f32[1,16]{1,0:T(1,128)S(1)}, f32[1,1]{1,0:T(1,128)}) custom-call(bf16[16,3584]{1,0:T(8,128)(2,1)} %hidden_hbm.1, bf16[384,3584]{1,0:T(8,128)(2,1)} %head_hbm.1, s32[1,16]{1,0:T(1,128)} %bitcast.4), custom_call_target="tpu_custom_call" | custom-call | tf_op jit(solution)/shard_map/pallas_call | solution.py:255
  24.9 2.3 %shard_map.75 = (bf16[16,896]{1,0:T(8,128)(2,1)}, f32[96,3584]{1,0:T(8,128)}, f32[1,16]{1,0:T(1,128)}, f32[1,16]{1,0:T(1,128)}, f32[1,1]{1,0:T(1,128)}) custom-call(bf16[16,896]{1,0:T(8,128)(2,1)S(1)} %get-tuple-element.15.refs_0_, f32[96,3584]{1,0:T(8,128)S(1)} %get-tuple-element.16.refs_1_, f32[1,16]{1,0:T(1,128)S(1)} %get-tuple-element.17.refs_2_, ...), custom_call_target="tpu_custom_call" | custom-call | tf_op jit(solution)/shard_map/pallas_call | solution.py:265
